TPU v7x, 32 devices: a whole 2x2x4 slice. The times are simulated.
32 devices in a mesh: gx: 4 (over x, core), gy: 4 (over z), gz: 2 (over y).
Axes of the slice: x: 2, y: 2, z: 4, core: 2. Of those that a mesh axis runs over, the one named last changes fastest.
Arguments:
- grad_bucket: bfloat16 [32, 1, 3584, 1024], P(('gx', 'gy', 'gz')), may hold values from -72000 to 72000
- parameters: bfloat16 [1, 3584, 1024], P(None, ('gx', 'gy', 'gz')), may hold values from -4 to 4
- row_state: float32 [1, 3584], P(None, ('gx', 'gy', 'gz')), may hold values from 0.01 to 10
- column_state: float32 [1, 1024], replicated, may hold values from 0.01 to 10
Outputs:
- new_parameters: bfloat16 [1, 3584, 1024], P(None, ('gx', 'gy', 'gz'))
- row_next: float32 [1, 3584], P(None, ('gx', 'gy', 'gz'))
- column_next: float32 [1, 1024], replicated
- first_layer: bfloat16 [3584, 1024], replicated
All inputs are finite; a program needn't handle non-finite values.
Results may differ from a plain program's by a relative error of at most 0.011.
Values may be sent and summed in bfloat16 or wider, within the bound.
A program may use at most 128 MiB of HBM per device.

v0:
```python
import math

import jax
import jax.numpy as jnp
from jax import lax
from jax.sharding import PartitionSpec as P

beta_two = 0.8
step_size = 0.5


def shards(grad_bucket, parameters, row_state, column_state):
    local_grad = grad_bucket[0].astype(jnp.float32)
    layer_count, full_width, columns = local_grad.shape
    summed = lax.psum_scatter(local_grad, ("gx", "gy", "gz"), scatter_dimension=1, tiled=True)
    clip_level = 0.5 * math.sqrt(layer_count * full_width * columns)
    squares = summed * summed
    norm_square = lax.psum(jnp.sum(squares), ("gx", "gy", "gz"))
    factor = jnp.minimum(jnp.float32(1.0), clip_level / jnp.sqrt(norm_square + 1e-06))
    clipped = factor * summed
    clipped_square = clipped * clipped
    row_next = beta_two * row_state + (1.0 - beta_two) * jnp.mean(clipped_square, axis=2)
    column_part, row_total = lax.psum(
        (jnp.sum(clipped_square, axis=1), jnp.sum(row_next, axis=1)), ("gx", "gy", "gz")
    )
    column_next = beta_two * column_state + (1.0 - beta_two) * column_part / full_width
    row_average = row_total / full_width
    second = row_next[:, :, None] * column_next[:, None, :] / row_average[:, None, None]
    update = clipped / jnp.sqrt(second)
    new_parameters = (parameters.astype(jnp.float32) - step_size * update).astype(jnp.bfloat16)
    first_layer = lax.all_gather(new_parameters[0], ("gx", "gy", "gz"), axis=0, tiled=True)
    return (new_parameters, row_next, column_next, first_layer)


def solution(mesh):
    in_specs = (
        P(("gx", "gy", "gz"), None, None, None),
        P(None, ("gx", "gy", "gz"), None),
        P(None, ("gx", "gy", "gz")),
        P(),
    )
    out_specs = (P(None, ("gx", "gy", "gz"), None), P(None, ("gx", "gy", "gz")), P(), P())
    return jax.shard_map(shards, mesh=mesh, in_specs=in_specs, out_specs=out_specs, check_vma=False)
```

profile of v0, /device:TPU:0, one launch (start us, length us, event | category | flops | bytes accessed | tf_op | source)
XLA Modules:
  0.0 509.3 jit_solution(15247041771120566344)
XLA Ops:
  7.2 0.0 reduce-scatter.2.cloned.1.call-start
  7.2 10.2 %bitcast_convert_fusion = f32[1,3584,1024]{2,1,0:T(8,128)} fusion(bf16[1,1,3584,1024]{3,2,1,0:T(8,128)(2,1)} %param.4), kind=kLoop, calls=%fused_computation | loop fusion | flops 3670016 | bytes 22020096 | tf_op jit(solution)/shard_map/convert_element_type | solution.py:13
  17.4 0.0 copy-start.4
  17.4 0.0 copy-start.2
  17.4 0.0 copy-start
  17.4 0.0 reduce-scatter.2.cloned.1.call-update
  17.4 0.0 all-gather.3.cloned.1.call-start
  17.5 317.9 %reduce-scatter.2.cloned.1.call-done = f32[1,112,1024]{2,1,0:T(8,128)} async-done(((f32[1,3584,1024]{2,1,0:T(8,128)}), f32[1,112,1024]{2,1,0:T(8,128)}) %reduce-scatter.2.cloned.1.call-update) | async-done | bytes 458768 | tf_op jit(solution)/shard_map/reduce_scatter | solution.py:15
  335.3 1.7 multiply_reduce_fusion
  337.1 39.7 %psum.21 = f32[]{:T(128)} all-reduce(f32[]{:T(128)} %multiply_reduce_fusion), channel_id=1, replica_groups=mesh['gx'=4,'gy'=4,'gz'=2] {'gx','gy','gz'}, use_global_device_ids=true, to_apply=%region_2.0 | all-reduce | flops 1 | bytes 8 | tf_op jit(solution)/shard_map/psum | solution.py:18
  377.5 1.2 multiply_reduce_fusion.1
  378.7 0.0 copy-done.4
  378.7 0.6 fusion
  379.3 0.0 copy-start.3
  379.3 39.7 %all-reduce = (f32[1]{0:T(128)}, f32[1,1024]{1,0:T(1,128)S(1)}) all-reduce(f32[1]{0:T(128)} %bitcast.5, f32[1,1024]{1,0:T(1,128)S(1)} %bitcast.14), channel_id=1, replica_groups=mesh['gx'=4,'gy'=4,'gz'=2] {'gx','gy','gz'}, use_global_device_ids=true, to_apply=%region_7.0 | all-reduce | flops 1025 | bytes 8200 | tf_op jit(solution)/shard_map/psum | solution.py:23
  419.6 0.0 copy-done.2
  419.7 0.0 copy-start.1
  419.7 0.0 copy-done
  419.7 1.9 subtract_convert_fusion
  421.6 0.0 all-gather.3.cloned.1.call-update
  421.6 73.8 %all-gather.3.cloned.1.call-done = bf16[1,3584,1024]{2,1,0:T(8,128)(2,1)} async-done(((bf16[1,112,1024]{2,1,0:T(8,128)(2,1)}), bf16[1,3584,1024]{2,1,0:T(8,128)(2,1)}) %all-gather.3.cloned.1.call-update) | async-done | bytes 7340048 | tf_op jit(solution)/shard_map/all_gather | solution.py:31
  495.4 7.0 %copy.9 = bf16[3584,1024]{1,0:T(8,128)(2,1)} copy(bf16[3584,1024]{1,0:T(8,128)(2,1)} %bitcast.12) | data formatting | bytes 14680064
  502.4 0.0 copy-done.3
  502.4 0.0 copy-done.1
  (1 shorter events, 0.0 us)
Async XLA Ops:
  7.2 328.2 %reduce-scatter.2.cloned.1.call-start = ((), (), s32[]{:S(2)}) async-start(), calls=%async_computation.1 | async-start | bytes 15138816 | tf_op jit(solution)/shard_map/reduce_scatter | solution.py:15
  17.4 361.3 %copy-start.4 = (f32[1,112]{1,0:T(1,128)S(1)}, f32[1,112]{1,0:T(1,128)}, u32[]{:S(2)}) copy-start(f32[1,112]{1,0:T(1,128)} %param.6) | copy-start | bytes 1348
  17.4 402.2 %copy-start.2 = (f32[1,1024]{1,0:T(1,128)S(1)}, f32[1,1024]{1,0:T(1,128)}, u32[]{:S(2)}) copy-start(f32[1,1024]{1,0:T(1,128)} %param.7) | copy-start | bytes 12292
  17.4 402.3 %copy-start = (bf16[1,112,1024]{2,1,0:T(8,128)(2,1)S(1)}, bf16[1,112,1024]{2,1,0:T(8,128)(2,1)}, u32[]{:S(2)}) copy-start(bf16[1,112,1024]{2,1,0:T(8,128)(2,1)} %param.5) | copy-start | bytes 688132
  17.4 478.0 %all-gather.3.cloned.1.call-start = ((), (), s32[]{:S(2)}) async-start(), calls=%async_computation.2 | async-start | bytes 7569408 | tf_op jit(solution)/shard_map/all_gather | solution.py:31
  379.3 123.1 %copy-start.3 = (f32[1,112]{1,0:T(1,128)}, f32[1,112]{1,0:T(1,128)S(1)}, u32[]{:S(2)}) copy-start(f32[1,112]{1,0:T(1,128)S(1)} %get-tuple-element.15) | copy-start | bytes 1348
  419.7 82.8 %copy-start.1 = (f32[1,1024]{1,0:T(1,128)}, f32[1,1024]{1,0:T(1,128)S(1)}, u32[]{:S(2)}) copy-start(f32[1,1024]{1,0:T(1,128)S(1)} %multiply_add_fusion) | copy-start | bytes 12292
Sparse Core Ops, SparseCore 0:
  17.5 317.7 reduce-scatter.1
  421.7 73.6 all-gather.2
where the time goes:
time: 510 us; the launch traced here: 509 us
  waiting for transfers between devices  392 us (77%)
  blocking collectives  79.4 us (16%)
  other arithmetic  15.6 us (3%)
  between operations  15.4 us (3%)
  local copies, waits for them, and re-layouts  6.99 us (1%)
    reduce_scatter x1, waiting for transfers between devices, shards(): lax.psum_scatter(local_grad, ('gx', 'gy', 'gz'), scatter_dimension=1, til...  318 us
    all_gather x1, waiting for transfers between devices, shards(): lax.all_gather(new_parameters[0], ('gx', 'gy', 'gz'), axis=0, tiled=True)  73.8 us
    psum x1, blocking collectives, shards(): norm_square = lax.psum(jnp.sum(squares), ('gx', 'gy', 'gz'))  39.7 us
    psum x1, blocking collectives, shards(): lax.psum((jnp.sum(clipped_square, axis=1), jnp.sum(row_next, axis=1)), ('...  39.7 us
  transfers between devices with their start and end apart: 2, of which 2 were waited for; matrix products, arithmetic and copies ran while one was open for 0% of the time, Pallas kernels for 0%

commit v1 on v0

v1 whole, which is shorter than its diff:
```python
import functools
import math

import jax
import jax.numpy as jnp
from jax import lax
from jax.experimental import pallas as pl
from jax.experimental.pallas import tpu as pltpu
from jax.sharding import PartitionSpec as P

beta_two = 0.8
step_size = 0.5
AXES = ("gx", "gy", "gz")
TILE = 16


def shards(grad_bucket, parameters, row_state, column_state):
    local_grad = grad_bucket[0].astype(jnp.float32)
    layer_count, full_width, columns = local_grad.shape
    summed = lax.psum_scatter(local_grad, AXES, scatter_dimension=1, tiled=True)
    clip_level = 0.5 * math.sqrt(layer_count * full_width * columns)
    squares = summed * summed
    norm_square = lax.psum(jnp.sum(squares), AXES)
    factor = jnp.minimum(jnp.float32(1.0), clip_level / jnp.sqrt(norm_square + 1e-06))
    clipped = factor * summed
    clipped_square = clipped * clipped
    row_next = beta_two * row_state + (1.0 - beta_two) * jnp.mean(clipped_square, axis=2)
    column_part, row_total = lax.psum((jnp.sum(clipped_square, axis=1), jnp.sum(row_next, axis=1)), AXES)
    column_next = beta_two * column_state + (1.0 - beta_two) * column_part / full_width
    row_average = row_total / full_width
    second = row_next[:, :, None] * column_next[:, None, :] / row_average[:, None, None]
    update = clipped / jnp.sqrt(second)
    new_parameters = (parameters.astype(jnp.float32) - step_size * update).astype(jnp.bfloat16)
    first_layer = lax.all_gather(new_parameters[0], AXES, axis=0, tiled=True)
    return (new_parameters, row_next, column_next, first_layer)


def flip(index, mask, size):
    out, bit = 0, 1
    while bit < size:
        out = out + bit * (((index // bit) % 2 + (mask // bit) % 2) % 2)
        bit *= 2
    return out


def kernel(nx, nz, grad, params, row_state, col_state, new_ref, row_ref, col_ref, full,
           lg, cr, r1a, r1b, r2a, r2b, rz, summed, own, st, st1, tot, st2,
           lsem, cs, crv, p1as, p1ar, p1bs, p1br, p2as, p2ar, p2bs, p2br, zs, zr,
           s1s, s1r, s2s, s2r, gzs, gzr, q1as, q1ar, q1bs, q1br, q2as, q2ar, q2bs, q2br, gcs, gcr):
    gx, z, y = lax.axis_index("gx"), lax.axis_index("gy"), lax.axis_index("gz")
    x, c = gx // 2, gx % 2
    rows, columns = params.shape
    half = columns // 2
    full_width = rows * 4 * nz * 2
    core_peer = (x * 2 + 1 - c, z, y)
    x_peer = ((1 - x) * 2 + c, z, y)
    y_peer = (gx, z, 1 - y)
    lo, hi = pl.ds(0, half), pl.ds(half, half)
    tiles = rows // TILE

    def zof(t):
        return flip(z, t, nz)

    def rdma(src, dst, ssem, rsem, peer):
        return pltpu.make_async_remote_copy(
            src_ref=src, dst_ref=dst, send_sem=ssem, recv_sem=rsem,
            device_id=peer, device_id_type=pl.DeviceIdType.MESH)

    rs_order = list(range(nz - 1, -1, -1))
    if nz == 4:
        rs_order = [2, 3, 1, 0]
    loads = {t: pltpu.make_async_copy(grad.at[:, c, zof(t)], lg.at[t], lsem.at[t]) for t in rs_order}
    for t in rs_order:
        loads[t].start()

    barrier = pltpu.get_barrier_semaphore()
    plane = [((gx + a) % nx, z, (y + b) % 2) for a in range(nx) for b in range(2) if (a, b) != (0, 0)]
    line = [(gx, zof(t), y) for t in range(1, nz)]
    for peer in plane + line:
        pl.semaphore_signal(barrier, inc=1, device_id=peer, device_id_type=pl.DeviceIdType.MESH)
    pl.semaphore_wait(barrier, len(plane) + len(line))

    core = {t: rdma(grad.at[:, 1 - c, zof(t)], cr.at[t], cs.at[t], crv.at[t], core_peer) for t in rs_order}
    for t in rs_order:
        core[t].start()
    p1a = {t: rdma(lg.at[t, 1 - x, :, :, lo], r1a.at[t], p1as.at[t], p1ar.at[t], x_peer) for t in rs_order}
    p1b = {t: rdma(lg.at[t, :, 1 - y, :, hi], r1b.at[t], p1bs.at[t], p1br.at[t], y_peer) for t in rs_order}
    p2a = {t: rdma(lg.at[t, x, 1 - y, :, lo], r2a.at[t], p2as.at[t], p2ar.at[t], y_peer) for t in rs_order}
    p2b = {t: rdma(lg.at[t, 1 - x, y, :, hi], r2b.at[t], p2bs.at[t], p2br.at[t], x_peer) for t in rs_order}
    zc = {t: rdma(lg.at[t, x, y], rz.at[t], zs.at[t], zr.at[t], (gx, zof(t), y)) for t in range(1, nz)}

    def add(a, b):
        return (a.astype(jnp.float32) + b.astype(jnp.float32)).astype(jnp.bfloat16)

    def stage_core(t):
        loads[t].wait()
        core[t].wait_recv()

        @pl.loop(0, tiles)
        def _(i):
            r = pl.ds(pl.multiple_of(i * TILE, TILE), TILE)
            for a in range(2):
                for b in range(2):
                    lg[t, a, b, r, :] = add(lg[t, a, b, r, :], cr[t, a, b, r, :])
        p1a[t].start()
        p1b[t].start()

    def stage_one(t):
        p1a[t].wait_recv()
        p1b[t].wait_recv()

        @pl.loop(0, tiles)
        def _(i):
            r = pl.ds(pl.multiple_of(i * TILE, TILE), TILE)
            for b in range(2):
                lg[t, x, b, r, lo] = add(lg[t, x, b, r, lo], r1a[t, b, r, :])
                lg[t, b, y, r, hi] = add(lg[t, b, y, r, hi], r1b[t, b, r, :])
        p2a[t].start()
        p2b[t].start()

    def stage_two(t):
        p2a[t].wait_recv()
        p2b[t].wait_recv()
        if t == 0:
            return

        @pl.loop(0, tiles)
        def _(i):
            r = pl.ds(pl.multiple_of(i * TILE, TILE), TILE)
            lg[t, x, y, r, lo] = add(lg[t, x, y, r, lo], r2a[t, r, :])
            lg[t, x, y, r, hi] = add(lg[t, x, y, r, hi], r2b[t, r, :])
        zc[t].start()

    n = len(rs_order)
    stage_core(rs_order[0])
    stage_core(rs_order[1])
    for i in range(n + 1):
        if i < n:
            stage_one(rs_order[i])
        if i + 2 < n:
            stage_core(rs_order[i + 2])
        if i >= 1:
            stage_two(rs_order[i - 1])
    for t in rs_order:
        if t:
            zc[t].wait_recv()

    def final(i, carry):
        r = pl.ds(pl.multiple_of(i * TILE, TILE), TILE)
        f32 = jnp.float32
        left = lg[0, x, y, r, lo].astype(f32) + r2a[0, r, :].astype(f32)
        right = lg[0, x, y, r, hi].astype(f32) + r2b[0, r, :].astype(f32)
        for t in range(1, nz):
            left = left + rz[t, r, lo].astype(f32)
            right = right + rz[t, r, hi].astype(f32)
        summed[r, lo] = left
        summed[r, hi] = right
        left, right = left * left, right * right
        own[r, :] = jnp.sum(left, axis=1, keepdims=True) + jnp.sum(right, axis=1, keepdims=True)
        return (carry[0] + left, carry[1] + right)

    zero = jnp.zeros((TILE, half), jnp.float32)
    left, right = lax.fori_loop(0, tiles, final, (zero, zero))
    st[0:1, lo] = jnp.sum(left, axis=0, keepdims=True)
    st[0:1, hi] = jnp.sum(right, axis=0, keepdims=True)
    st[1:2, :] = jnp.broadcast_to(jnp.sum(row_state[...], axis=1, keepdims=True), (1, columns))

    me = gx * 2 + y
    sends = []
    for k, (a, b) in enumerate([(a, b) for a in range(nx) for b in range(2) if (a, b) != (0, 0)]):
        sends.append(rdma(st, st1.at[me], s1s.at[k], s1r.at[k], ((gx + a) % nx, z, (y + b) % 2)))
        sends[-1].start()
    st1[me] = st[...]
    for copy in sends:
        copy.wait_recv()
    total = st1[0]
    for k in range(1, nx * 2):
        total = total + st1[k]
    tot[...] = total
    line_sends = []
    for t in range(1, nz):
        line_sends.append(rdma(tot, st2.at[z], s2s.at[t], s2r.at[t], (gx, zof(t), y)))
        line_sends[-1].start()
    st2[z] = total
    for t in rs_order:
        core[t].wait_send()
        for copy in (p1a[t], p1b[t], p2a[t], p2b[t]):
            copy.wait_send()
        if t:
            zc[t].wait_send()
    for copy in line_sends:
        copy.wait_recv()
    total = st2[0]
    for k in range(1, nz):
        total = total + st2[k]
    column_sum = total[0:1, :]
    norm_square = jnp.sum(column_sum, axis=1, keepdims=True)
    state_sum = total[1:2, 0:1]
    clip_level = 0.5 * math.sqrt(full_width * columns)
    factor = jnp.minimum(jnp.float32(1.0), clip_level / jnp.sqrt(norm_square + 1e-06))
    square_factor = factor * factor
    column_next = beta_two * col_state[...] + (1.0 - beta_two) * (square_factor * column_sum / full_width)
    col_ref[...] = column_next
    row_average = (beta_two * state_sum + (1.0 - beta_two) * (square_factor * norm_square / columns)) / full_width
    diagonal = lax.broadcasted_iota(jnp.int32, (rows, rows), 0) == lax.broadcasted_iota(jnp.int32, (rows, rows), 1)
    state_down = jnp.sum(jnp.where(diagonal, jnp.broadcast_to(row_state[...], (rows, rows)), 0.0), axis=1, keepdims=True)
    row_next = beta_two * state_down + (1.0 - beta_two) * (square_factor * own[...] / columns)
    row_ref[...] = jnp.sum(jnp.where(diagonal, jnp.broadcast_to(row_next, (rows, rows)), 0.0), axis=0, keepdims=True)
    own[...] = (step_size * factor) / jnp.sqrt(row_next / row_average)
    col_scale = 1.0 / jnp.sqrt(column_next)

    @pl.loop(0, tiles)
    def _(i):
        r = pl.ds(pl.multiple_of(i * TILE, TILE), TILE)
        new = params[r, :].astype(jnp.float32) - (summed[r, :] * own[r, :]) * col_scale
        new = new.astype(jnp.bfloat16)
        full[x, c, z, y, r, :] = new
        new_ref[r, :] = new

    gz = {t: rdma(full.at[x, c, z, y], full.at[x, c, z, y], gzs.at[t], gzr.at[t], (gx, zof(t), y)) for t in range(1, nz)}

    def same(view, ssem, rsem, peer):
        return rdma(view, view, ssem, rsem, peer)

    q1a, q1b, q2a, q2b, gc = {}, {}, {}, {}, {}
    for t in range(nz):
        u = zof(t)
        q1a[t] = same(full.at[x, c, u, y, :, lo], q1as.at[t], q1ar.at[t], y_peer)
        q1b[t] = same(full.at[x, c, u, y, :, hi], q1bs.at[t], q1br.at[t], x_peer)
        q2a[t] = same(full.at[x, c, u, :, :, lo], q2as.at[t], q2ar.at[t], x_peer)
        q2b[t] = same(full.at[:, c, u, y, :, hi], q2bs.at[t], q2br.at[t], y_peer)
        gc[t] = same(full.at[:, c, u], gcs.at[t], gcr.at[t], core_peer)

    def gather_one(t):
        if t:
            gz[t].wait_recv()
        q1a[t].start()
        q1b[t].start()

    def gather_two(t):
        q1a[t].wait_recv()
        q1b[t].wait_recv()
        q2a[t].start()
        q2b[t].start()

    def gather_core(t):
        q2a[t].wait_recv()
        q2b[t].wait_recv()
        gc[t].start()

    q1a[0].start()
    q1b[0].start()
    for t in range(1, nz):
        gz[t].start()
    gather_two(0)
    for t in range(1, nz):
        gather_one(t)
        gather_core(t - 1)
        gather_two(t)
    gather_core(nz - 1)
    for copy in sends + line_sends:
        copy.wait_send()
    for t in range(nz):
        if t:
            gz[t].wait_send()
        for copy in (q1a[t], q1b[t], q2a[t], q2b[t]):
            copy.wait_send()
        gc[t].wait_send()
        gc[t].wait_recv()


def fused(nx, nz, grad_bucket, parameters, row_state, column_state):
    _, _, full_width, columns = grad_bucket.shape
    rows = parameters.shape[1]
    half = columns // 2
    bf16, f32 = jnp.bfloat16, jnp.float32
    vmem = pl.BlockSpec(memory_space=pltpu.VMEM)
    dma = pltpu.SemaphoreType.DMA
    new, row, col, full = pl.pallas_call(
        functools.partial(kernel, nx, nz),
        out_shape=(
            jax.ShapeDtypeStruct((rows, columns), bf16),
            jax.ShapeDtypeStruct((1, rows), f32),
            jax.ShapeDtypeStruct((1, columns), f32),
            jax.ShapeDtypeStruct((2, 2, nz, 2, rows, columns), bf16),
        ),
        in_specs=[pl.BlockSpec(memory_space=pl.ANY), vmem, vmem, vmem],
        out_specs=(vmem, vmem, vmem, vmem),
        scratch_shapes=[
            pltpu.VMEM((nz, 2, 2, rows, columns), bf16),
            pltpu.VMEM((nz, 2, 2, rows, columns), bf16),
            pltpu.VMEM((nz, 2, rows, half), bf16),
            pltpu.VMEM((nz, 2, rows, half), bf16),
            pltpu.VMEM((nz, rows, half), bf16),
            pltpu.VMEM((nz, rows, half), bf16),
            pltpu.VMEM((nz, rows, columns), bf16),
            pltpu.VMEM((rows, columns), f32),
            pltpu.VMEM((rows, 1), f32),
            pltpu.VMEM((2, columns), f32),
            pltpu.VMEM((nx * 2, 2, columns), f32),
            pltpu.VMEM((2, columns), f32),
            pltpu.VMEM((nz, 2, columns), f32),
        ] + [dma((nz,))] * 13 + [dma((nx * 2,))] * 2 + [dma((nz,))] * 14,
        compiler_params=pltpu.CompilerParams(
            collective_id=0, has_side_effects=True, vmem_limit_bytes=48 * 1024 * 1024),
    )(grad_bucket.reshape(2, 2, nz, 2, rows, columns), parameters[0], row_state, column_state)
    return (new[None], row, col, full.reshape(full_width, columns))


def solution(mesh):
    nx, nz, ny = (mesh.shape[a] for a in AXES)
    in_specs = (
        P(AXES, None, None, None),
        P(None, AXES, None),
        P(None, AXES),
        P(),
    )
    out_specs = (P(None, AXES, None), P(None, AXES), P(), P())
    fits = nx == 4 and ny == 2 and nz & (nz - 1) == 0

    def body(grad_bucket, parameters, row_state, column_state):
        if fits and grad_bucket.shape[1] == 1 and parameters.shape[1] % TILE == 0:
            return fused(nx, nz, grad_bucket, parameters, row_state, column_state)
        return shards(grad_bucket, parameters, row_state, column_state)

    return jax.shard_map(body, mesh=mesh, in_specs=in_specs, out_specs=out_specs, check_vma=False)
```

time: 510 us -> 107 us (0.21)
  waiting for transfers between devices: 392 us -> 0 us
  Pallas kernels: 0 us -> 94.7 us
  blocking collectives: 79.4 us -> 0 us
  other arithmetic: 15.6 us -> 0 us
  between operations: 15.4 us -> 0.65 us
    reduce_scatter x1 -> x0, waiting for transfers between devices: 318 us -> none  [shards(): lax.psum_scatter(local_grad, ('gx', 'gy', 'gz'), scatter_dimension=1, til...]
    pallas_call x0 -> x1, Pallas kernels: none -> 94.7 us  [fused(): pl.pallas_call(functools.partial(kernel, nx, nz), out_shape=(jax.ShapeDty...]
    psum x2 -> x0, blocking collectives: 79.4 us -> none  [the longest x1 39.7 us: shards(): norm_square = lax.psum(jnp.sum(squares), ('gx', 'gy', 'gz'))]
    all_gather x1 -> x0, waiting for transfers between devices: 73.8 us -> none  [shards(): lax.all_gather(new_parameters[0], ('gx', 'gy', 'gz'), axis=0, tiled=True)]
    convert_element_type x2 -> x0, other arithmetic: 12.1 us -> none  [the longest x1 10.2 us: shards(): local_grad = grad_bucket[0].astype(jnp.float32)]
    unnamed x11 -> x10, local copies, waits for them, and re-layouts: 6.99 us -> 11 us
  transfers between devices with their start and end apart: 2 -> 0, of which waited for: 2 -> 0; matrix products, arithmetic and copies ran while one was open for 0% -> 0% of each run, Pallas kernels for 0% -> 0%
where the time goes in v1:
time: 107 us; the launch traced here: 106 us
  Pallas kernels  94.7 us (89%)
  local copies, waits for them, and re-layouts  11 us (10%)
    pallas_call x1, Pallas kernels, fused(): pl.pallas_call(functools.partial(kernel, nx, nz), out_shape=(jax.ShapeDty...  94.7 us
    unnamed x10, local copies, waits for them, and re-layouts  11 us

profile of v1, /device:TPU:0, one launch (start us, length us, event | category | flops | bytes accessed | tf_op | source)
XLA Modules:
  0.0 106.4 jit_solution(3258016538922104673)
XLA Ops:
  0.6 0.0 copy-start
  0.6 0.9 copy-done
  1.6 0.0 copy-start.1
  1.6 0.7 copy-done.1
  2.3 0.0 copy-start.2
  2.3 0.7 copy-done.2
  2.9 94.7 %shard_map.75 = (bf16[112,1024]{1,0:T(8,128)(2,1)S(1)}, f32[1,112]{1,0:T(1,128)S(1)}, f32[1,1024]{1,0:T(1,128)S(1)}, bf16[2,2,4,2,112,1024]{5,4,3,2,1,0:T(8,128)(2,1)}) custom-call(bf16[2,2,4,2,112,1024]{5,4,3,2,1,0:T(8,128)(2,1)} %bitcast.6, bf16[112,1024]{1,0:T(8,128)(2,1)S(1)} %bitcast.5, f32[1,112]{1,0:T(1,128)S(1)} %copy-done.2, f32[1,1024]{1,0:T(1,128)S(1)} %copy-done.1), custom_call_target="tpu_custom_call" | custom-call | tf_op jit(solution)/shard_map/pallas_call | solution.py:279
  97.6 0.7 copy.12
  98.3 0.5 copy.13
  98.8 0.6 copy.14
  99.4 7.0 %copy.15 = bf16[3584,1024]{1,0:T(8,128)(2,1)} copy(bf16[3584,1024]{1,0:T(8,128)(2,1)} %bitcast.7) | data formatting | bytes 14680064
Async XLA Ops:
  0.6 0.9 copy-start
  1.6 0.7 copy-start.1
  2.3 0.7 copy-start.2

commit v2 on v1

v2 whole, which is shorter than its diff:
```python
import functools
import math

import jax
import jax.numpy as jnp
from jax import lax
from jax.experimental import pallas as pl
from jax.experimental.pallas import tpu as pltpu
from jax.sharding import PartitionSpec as P

beta_two = 0.8
step_size = 0.5
AXES = ("gx", "gy", "gz")
TILE = 16
VMEM_BYTES = 67043328 - 131072


def shards(grad_bucket, parameters, row_state, column_state):
    local_grad = grad_bucket[0].astype(jnp.float32)
    layer_count, full_width, columns = local_grad.shape
    summed = lax.psum_scatter(local_grad, AXES, scatter_dimension=1, tiled=True)
    clip_level = 0.5 * math.sqrt(layer_count * full_width * columns)
    squares = summed * summed
    norm_square = lax.psum(jnp.sum(squares), AXES)
    factor = jnp.minimum(jnp.float32(1.0), clip_level / jnp.sqrt(norm_square + 1e-06))
    clipped = factor * summed
    clipped_square = clipped * clipped
    row_next = beta_two * row_state + (1.0 - beta_two) * jnp.mean(clipped_square, axis=2)
    column_part, row_total = lax.psum((jnp.sum(clipped_square, axis=1), jnp.sum(row_next, axis=1)), AXES)
    column_next = beta_two * column_state + (1.0 - beta_two) * column_part / full_width
    row_average = row_total / full_width
    second = row_next[:, :, None] * column_next[:, None, :] / row_average[:, None, None]
    update = clipped / jnp.sqrt(second)
    new_parameters = (parameters.astype(jnp.float32) - step_size * update).astype(jnp.bfloat16)
    first_layer = lax.all_gather(new_parameters[0], AXES, axis=0, tiled=True)
    return (new_parameters, row_next, column_next, first_layer)


def flip(index, mask, size):
    out, bit = 0, 1
    while bit < size:
        out = out + bit * (((index // bit) % 2 + (mask // bit) % 2) % 2)
        bit *= 2
    return out


def kernel(nx, nz, grad, params_in, row_in, col_in, new_ref, row_ref, col_ref, full,
           lg, cr, r1a, r1b, r2a, r2b, rz, summed, own, st, st1, tot, st2, params, row_state, col_state,
           lsem, isem, cs, crv, fas, far, fbs, fbr, gas, gar, gbs, gbr, has, har, hbs, hbr, zs, zr,
           s1s, s1r, s2s, s2r, gzs, gzr, q1as, q1ar, q1bs, q1br, q2as, q2ar, q2bs, q2br,
           q3as, q3ar, q3bs, q3br, gcs, gcr):
    gx, z, y = lax.axis_index("gx"), lax.axis_index("gy"), lax.axis_index("gz")
    x, c = gx // 2, gx % 2
    rows, columns = params.shape
    half = columns // 2
    full_width = rows * 4 * nz * 2
    core_peer = (x * 2 + 1 - c, z, y)
    x_peer = ((1 - x) * 2 + c, z, y)
    y_peer = (gx, z, 1 - y)
    lo, hi = pl.ds(0, half), pl.ds(half, half)
    tiles = rows // TILE
    f32 = jnp.float32
    blocks = [(1 - x, 1 - y), (1 - x, y), (x, 1 - y), (x, y)]

    def zof(t):
        return flip(z, t, nz)

    def rdma(src, dst, ssem, rsem, peer):
        return pltpu.make_async_remote_copy(
            src_ref=src, dst_ref=dst, send_sem=ssem, recv_sem=rsem,
            device_id=peer, device_id_type=pl.DeviceIdType.MESH)

    rs_order = [2, 3, 1, 0] if nz == 4 else list(range(nz - 1, -1, -1))
    loads = {t: pltpu.make_async_copy(grad.at[:, c, zof(t)], lg.at[t], lsem.at[t]) for t in rs_order}
    for t in rs_order:
        loads[t].start()
    small = [pltpu.make_async_copy(src, dst, isem.at[k]) for k, (src, dst) in enumerate(
        [(params_in, params), (row_in, row_state), (col_in, col_state)])]
    for copy in small:
        copy.start()

    barrier = pltpu.get_barrier_semaphore()
    plane = [((gx + a) % nx, z, (y + b) % 2) for a in range(nx) for b in range(2) if (a, b) != (0, 0)]
    line = [(gx, zof(t), y) for t in range(1, nz)]
    for peer in line + plane:
        pl.semaphore_signal(barrier, inc=1, device_id=peer, device_id_type=pl.DeviceIdType.MESH)
    pl.semaphore_wait(barrier, len(plane) + len(line))

    core, fa, fb, ga, gb, ha, hb, zc = {}, {}, {}, {}, {}, {}, {}, {}
    for t in rs_order:
        for k, (bx, by) in enumerate(blocks):
            core[t, k] = rdma(grad.at[bx, 1 - c, zof(t), by], cr.at[t, k], cs.at[t, k], crv.at[t, k], core_peer)
            core[t, k].start()
        fa[t] = rdma(lg.at[t, 1 - x, 1 - y, :, lo], r1a.at[t, 0], fas.at[t], far.at[t], x_peer)
        fb[t] = rdma(lg.at[t, 1 - x, 1 - y, :, hi], r1b.at[t, 0], fbs.at[t], fbr.at[t], y_peer)
        ga[t] = rdma(lg.at[t, 1 - x, y, :, lo], r1a.at[t, 1], gas.at[t], gar.at[t], x_peer)
        gb[t] = rdma(lg.at[t, x, 1 - y, :, hi], r1b.at[t, 1], gbs.at[t], gbr.at[t], y_peer)
        ha[t] = rdma(lg.at[t, x, 1 - y, :, lo], r2a.at[t], has.at[t], har.at[t], y_peer)
        hb[t] = rdma(lg.at[t, 1 - x, y, :, hi], r2b.at[t], hbs.at[t], hbr.at[t], x_peer)
        if t:
            zc[t] = rdma(lg.at[t, x, y], rz.at[t], zs.at[t], zr.at[t], (gx, zof(t), y))

    def add(*terms):
        total = terms[0].astype(f32)
        for term in terms[1:]:
            total = total + term.astype(f32)
        return total

    def over_rows(step):
        @pl.loop(0, tiles)
        def _(i):
            step(pl.ds(pl.multiple_of(i * TILE, TILE), TILE))

    def stage_core(t):
        loads[t].wait()
        for k, (bx, by) in enumerate(blocks):
            core[t, k].wait_recv()

            def step(r):
                lg[t, bx, by, r, :] = add(lg[t, bx, by, r, :], cr[t, k, r, :]).astype(jnp.bfloat16)
            over_rows(step)
            if k == 0:
                fa[t].start()
                fb[t].start()
            elif k == 1:
                ga[t].start()
            elif k == 2:
                gb[t].start()

    def stage_first(t):
        fa[t].wait_recv()
        fb[t].wait_recv()

        def step(r):
            lg[t, x, 1 - y, r, lo] = add(lg[t, x, 1 - y, r, lo], r1a[t, 0, r, :]).astype(jnp.bfloat16)
            lg[t, 1 - x, y, r, hi] = add(lg[t, 1 - x, y, r, hi], r1b[t, 0, r, :]).astype(jnp.bfloat16)
        over_rows(step)
        ha[t].start()
        hb[t].start()

    def stage_second(t):
        for copy in (ga[t], gb[t], ha[t], hb[t]):
            copy.wait_recv()
        if t == 0:
            return

        def step(r):
            lg[t, x, y, r, lo] = add(lg[t, x, y, r, lo], r1a[t, 1, r, :], r2a[t, r, :]).astype(jnp.bfloat16)
            lg[t, x, y, r, hi] = add(lg[t, x, y, r, hi], r1b[t, 1, r, :], r2b[t, r, :]).astype(jnp.bfloat16)
        over_rows(step)
        zc[t].start()

    stage_core(rs_order[0])
    for i, t in enumerate(rs_order):
        stage_first(t)
        if i + 1 < nz:
            stage_core(rs_order[i + 1])
        stage_second(t)
    for t in rs_order:
        if t:
            zc[t].wait_recv()
    for copy in small:
        copy.wait()

    def final(i, carry):
        r = pl.ds(pl.multiple_of(i * TILE, TILE), TILE)
        left = add(lg[0, x, y, r, lo], r1a[0, 1, r, :], r2a[0, r, :], *[rz[t, r, lo] for t in range(1, nz)])
        right = add(lg[0, x, y, r, hi], r1b[0, 1, r, :], r2b[0, r, :], *[rz[t, r, hi] for t in range(1, nz)])
        summed[r, lo] = left
        summed[r, hi] = right
        left, right = left * left, right * right
        own[r, :] = jnp.sum(left, axis=1, keepdims=True) + jnp.sum(right, axis=1, keepdims=True)
        return (carry[0] + left, carry[1] + right)

    zero = jnp.zeros((TILE, half), f32)
    left, right = lax.fori_loop(0, tiles, final, (zero, zero))
    st[0:1, lo] = jnp.sum(left, axis=0, keepdims=True)
    st[0:1, hi] = jnp.sum(right, axis=0, keepdims=True)
    st[1:2, :] = jnp.broadcast_to(jnp.sum(row_state[...], axis=1, keepdims=True), (1, columns))

    me = gx * 2 + y
    sends = []
    for k, peer in enumerate(plane):
        sends.append(rdma(st, st1.at[me], s1s.at[k], s1r.at[k], peer))
        sends[-1].start()
    st1[me] = st[...]
    for t in rs_order:
        for k in range(len(blocks)):
            core[t, k].wait_send()
        for copy in (fa[t], fb[t], ga[t], gb[t], ha[t], hb[t]):
            copy.wait_send()
        if t:
            zc[t].wait_send()
    for copy in sends:
        copy.wait_recv()
    total = st1[0]
    for k in range(1, nx * 2):
        total = total + st1[k]
    tot[...] = total
    line_sends = []
    for t in range(1, nz):
        line_sends.append(rdma(tot, st2.at[z], s2s.at[t], s2r.at[t], (gx, zof(t), y)))
        line_sends[-1].start()
    st2[z] = total
    diagonal = lax.broadcasted_iota(jnp.int32, (rows, rows), 0) == lax.broadcasted_iota(jnp.int32, (rows, rows), 1)
    state_down = jnp.sum(jnp.where(diagonal, jnp.broadcast_to(row_state[...], (rows, rows)), 0.0), axis=1, keepdims=True)
    for copy in line_sends:
        copy.wait_recv()
    total = st2[0]
    for k in range(1, nz):
        total = total + st2[k]
    column_sum = total[0:1, :]
    norm_square = jnp.sum(column_sum, axis=1, keepdims=True)
    state_sum = total[1:2, 0:1]
    clip_level = 0.5 * math.sqrt(full_width * columns)
    factor = jnp.minimum(jnp.float32(1.0), clip_level / jnp.sqrt(norm_square + 1e-06))
    square_factor = factor * factor
    column_next = beta_two * col_state[...] + (1.0 - beta_two) * (square_factor * column_sum / full_width)
    row_average = (beta_two * state_sum + (1.0 - beta_two) * (square_factor * norm_square / columns)) / full_width
    row_next = beta_two * state_down + (1.0 - beta_two) * (square_factor * own[...] / columns)
    own[...] = (step_size * factor) / jnp.sqrt(row_next / row_average)
    col_scale = 1.0 / jnp.sqrt(column_next)

    def update(r):
        new = params[r, :].astype(f32) - (summed[r, :] * own[r, :]) * col_scale
        full[x, c, z, y, r, :] = new.astype(jnp.bfloat16)
    over_rows(update)

    def same(view, ssem, rsem, peer):
        return rdma(view, view, ssem, rsem, peer)

    gz, q1a, q1b, q2a, q2b, q3a, q3b, gc = {}, {}, {}, {}, {}, {}, {}, {}
    for t in range(nz):
        u = zof(t)
        if t:
            gz[t] = rdma(full.at[x, c, z, y], full.at[x, c, z, y], gzs.at[t], gzr.at[t], (gx, u, y))
        q1a[t] = same(full.at[x, c, u, y, :, lo], q1as.at[t], q1ar.at[t], y_peer)
        q1b[t] = same(full.at[x, c, u, y, :, hi], q1bs.at[t], q1br.at[t], x_peer)
        q2a[t] = same(full.at[x, c, u, y, :, lo], q2as.at[t], q2ar.at[t], x_peer)
        q2b[t] = same(full.at[x, c, u, y, :, hi], q2bs.at[t], q2br.at[t], y_peer)
        q3a[t] = same(full.at[x, c, u, 1 - y, :, lo], q3as.at[t], q3ar.at[t], x_peer)
        q3b[t] = same(full.at[1 - x, c, u, y, :, hi], q3bs.at[t], q3br.at[t], y_peer)
        for k, (bx, by) in enumerate(blocks):
            gc[t, k] = same(full.at[bx, c, u, by], gcs.at[t, k], gcr.at[t, k], core_peer)

    def gather_own(t):
        if t:
            gz[t].wait_recv()
        for copy in (q1a[t], q1b[t], q2a[t], q2b[t]):
            copy.start()
        gc[t, 3].start()

    def gather_cross(t):
        q1a[t].wait_recv()
        q1b[t].wait_recv()
        q3a[t].start()
        q3b[t].start()

    def gather_side(t):
        q2a[t].wait_recv()
        gc[t, 1].start()
        q2b[t].wait_recv()
        gc[t, 2].start()

    def gather_far(t):
        q3a[t].wait_recv()
        q3b[t].wait_recv()
        gc[t, 0].start()

    q1a[0].start()
    q1b[0].start()
    for t in range(1, nz):
        gz[t].start()
    q2a[0].start()
    q2b[0].start()
    gc[0, 3].start()
    new_ref[...] = full[x, c, z, y]
    col_ref[...] = column_next
    row_ref[...] = jnp.sum(jnp.where(diagonal, jnp.broadcast_to(row_next, (rows, rows)), 0.0), axis=0, keepdims=True)
    gather_cross(0)
    for t in range(1, nz):
        gather_own(t)
        gather_side(t - 1)
        gather_far(t - 1)
        gather_cross(t)
    gather_side(nz - 1)
    gather_far(nz - 1)
    for copy in sends + line_sends:
        copy.wait_send()
    for t in range(nz):
        if t:
            gz[t].wait_send()
        for copy in (q1a[t], q1b[t], q2a[t], q2b[t], q3a[t], q3b[t]):
            copy.wait_send()
        for k in range(len(blocks)):
            gc[t, k].wait_send()
            gc[t, k].wait_recv()


def write_out(*refs):
    count = (len(refs) - 1) // 2
    sem = refs[-1]
    copies = [pltpu.make_async_copy(refs[k], refs[count + k], sem.at[k]) for k in range(count)]
    for copy in copies:
        copy.start()
    for copy in copies:
        copy.wait()


def fused(nx, nz, grad_bucket, parameters, row_state, column_state):
    _, _, full_width, columns = grad_bucket.shape
    rows = parameters.shape[1]
    half = columns // 2
    bf16, f32 = jnp.bfloat16, jnp.float32
    vmem = pl.BlockSpec(memory_space=pltpu.VMEM)
    hbm = pl.BlockSpec(memory_space=pltpu.HBM)
    dma = pltpu.SemaphoreType.DMA
    shapes = [((rows, columns), bf16), ((1, rows), f32), ((1, columns), f32), ((2, 2, nz, 2, rows, columns), bf16)]
    held = 2 * columns * (rows + full_width) + 4 * (columns + -(-rows // 128) * 128)
    results = pl.pallas_call(
        functools.partial(kernel, nx, nz),
        out_shape=tuple(pltpu.VMEM(*shape) for shape in shapes),
        in_specs=[hbm] * 4,
        out_specs=(vmem,) * 4,
        scratch_shapes=[
            pltpu.VMEM((nz, 2, 2, rows, columns), bf16),
            pltpu.VMEM((nz, 4, rows, columns), bf16),
            pltpu.VMEM((nz, 2, rows, half), bf16),
            pltpu.VMEM((nz, 2, rows, half), bf16),
            pltpu.VMEM((nz, rows, half), bf16),
            pltpu.VMEM((nz, rows, half), bf16),
            pltpu.VMEM((nz, rows, columns), bf16),
            pltpu.VMEM((rows, columns), f32),
            pltpu.VMEM((rows, 1), f32),
            pltpu.VMEM((2, columns), f32),
            pltpu.VMEM((nx * 2, 2, columns), f32),
            pltpu.VMEM((2, columns), f32),
            pltpu.VMEM((nz, 2, columns), f32),
            pltpu.VMEM((rows, columns), bf16),
            pltpu.VMEM((1, rows), f32),
            pltpu.VMEM((1, columns), f32),
        ] + [dma((nz,)), dma((3,))] + [dma((nz, 4))] * 2 + [dma((nz,))] * 14
        + [dma((nx * 2,))] * 2 + [dma((nz,))] * 16 + [dma((nz, 4))] * 2,
        compiler_params=pltpu.CompilerParams(
            collective_id=0, has_side_effects=True, vmem_limit_bytes=VMEM_BYTES - held),
    )(grad_bucket.reshape(2, 2, nz, 2, rows, columns), parameters[0], row_state, column_state)
    new, row, col, full = pl.pallas_call(
        write_out,
        out_shape=tuple(jax.ShapeDtypeStruct(*shape) for shape in shapes),
        in_specs=[vmem] * 4,
        out_specs=(hbm,) * 4,
        scratch_shapes=[dma((4,))],
        compiler_params=pltpu.CompilerParams(vmem_limit_bytes=4 * 1024 * 1024),
    )(*[pltpu.with_memory_space_constraint(result, pltpu.VMEM) for result in results])
    return (new[None], row, col, full.reshape(full_width, columns))


def solution(mesh):
    nx, nz, ny = (mesh.shape[a] for a in AXES)
    in_specs = (
        P(AXES, None, None, None),
        P(None, AXES, None),
        P(None, AXES),
        P(),
    )
    out_specs = (P(None, AXES, None), P(None, AXES), P(), P())
    fits = nx == 4 and ny == 2 and nz & (nz - 1) == 0

    def body(grad_bucket, parameters, row_state, column_state):
        if fits and grad_bucket.shape[1] == 1 and parameters.shape[1] % TILE == 0:
            return fused(nx, nz, grad_bucket, parameters, row_state, column_state)
        return shards(grad_bucket, parameters, row_state, column_state)

    return jax.shard_map(body, mesh=mesh, in_specs=in_specs, out_specs=out_specs, check_vma=False)
```

time: 107 us -> 88 us (0.82)
  local copies, waits for them, and re-layouts: 11 us -> 0 us
  Pallas kernels: 94.7 us -> 87.2 us
    unnamed x10 -> x0, local copies, waits for them, and re-layouts: 11 us -> none
    pallas_call x1 -> x2, Pallas kernels: 94.7 us -> 87.2 us  [the longest x1 84 us: fused(): pl.pallas_call(functools.partial(kernel, nx, nz), out_shape=tuple((pltpu....]
where the time goes in v2:
time: 88 us; the launch traced here: 87.8 us
  Pallas kernels  87.2 us (99%)
    pallas_call x1, Pallas kernels, fused(): pl.pallas_call(functools.partial(kernel, nx, nz), out_shape=tuple((pltpu....  84 us
    pallas_call x1, Pallas kernels, fused(): pl.pallas_call(write_out, out_shape=tuple((jax.ShapeDtypeStruct(*shape) f...  3.17 us

profile of v2, /device:TPU:0, one launch (start us, length us, event | category | flops | bytes accessed | tf_op | source)
XLA Modules:
  0.0 87.8 jit_solution(17071687934967634230)
XLA Ops:
  0.6 84.0 %shard_map.75 = (bf16[112,1024]{1,0:T(8,128)(2,1)S(1)}, f32[1,112]{1,0:T(1,128)S(1)}, f32[1,1024]{1,0:T(1,128)S(1)}, bf16[2,2,4,2,112,1024]{5,4,3,2,1,0:T(8,128)(2,1)S(1)}) custom-call(bf16[2,2,4,2,112,1024]{5,4,3,2,1,0:T(8,128)(2,1)} %bitcast.4, bf16[112,1024]{1,0:T(8,128)(2,1)} %bitcast.5, f32[1,112]{1,0:T(1,128)} %row_in.1, f32[1,1024]{1,0:T(1,128)} %col_in.1), custom_call_target="tpu_custom_call" | custom-call | tf_op jit(solution)/shard_map/pallas_call | solution.py:320
  84.7 3.2 %shard_map.76 = (bf16[112,1024]{1,0:T(8,128)(2,1)}, f32[1,112]{1,0:T(1,128)}, f32[1,1024]{1,0:T(1,128)}, bf16[2,2,4,2,112,1024]{5,4,3,2,1,0:T(8,128)(2,1)}) custom-call(bf16[112,1024]{1,0:T(8,128)(2,1)S(1)} %get-tuple-element.12.refs_0_, f32[1,112]{1,0:T(1,128)S(1)} %get-tuple-element.13.refs_1_, f32[1,1024]{1,0:T(1,128)S(1)} %get-tuple-element.14.refs_2_, ...), custom_call_target="tpu_custom_call" | custom-call | tf_op jit(solution)/shard_map/pallas_call | solution.py:347

commit v3 on v2

--- a/solution.py
+++ b/solution.py
@@ -155,17 +155,27 @@
         stage_first(t)
         if i + 1 < nz:
             stage_core(rs_order[i + 1])
+        else:
+            for copy in small:
+                copy.wait()
+            st[1:2, :] = jnp.broadcast_to(jnp.sum(row_state[...], axis=1, keepdims=True), (1, columns))
+            early = [k for k in rs_order[:-2] if k]
+            for k in early:
+                zc[k].wait_recv()
+
+            def gathered(r):
+                summed[r, :] = add(lg[0, x, y, r, :], *[rz[k, r, :] for k in early])
+            over_rows(gathered)
         stage_second(t)
-    for t in rs_order:
+    for t in rs_order[-2:]:
         if t:
             zc[t].wait_recv()
-    for copy in small:
-        copy.wait()
+    late = [t for t in rs_order[-2:] if t]
 
     def final(i, carry):
         r = pl.ds(pl.multiple_of(i * TILE, TILE), TILE)
-        left = add(lg[0, x, y, r, lo], r1a[0, 1, r, :], r2a[0, r, :], *[rz[t, r, lo] for t in range(1, nz)])
-        right = add(lg[0, x, y, r, hi], r1b[0, 1, r, :], r2b[0, r, :], *[rz[t, r, hi] for t in range(1, nz)])
+        left = add(summed[r, lo], r1a[0, 1, r, :], r2a[0, r, :], *[rz[t, r, lo] for t in late])
+        right = add(summed[r, hi], r1b[0, 1, r, :], r2b[0, r, :], *[rz[t, r, hi] for t in late])
         summed[r, lo] = left
         summed[r, hi] = right
         left, right = left * left, right * right
@@ -176,7 +186,6 @@
     left, right = lax.fori_loop(0, tiles, final, (zero, zero))
     st[0:1, lo] = jnp.sum(left, axis=0, keepdims=True)
     st[0:1, hi] = jnp.sum(right, axis=0, keepdims=True)
-    st[1:2, :] = jnp.broadcast_to(jnp.sum(row_state[...], axis=1, keepdims=True), (1, columns))
 
     me = gx * 2 + y
     sends = []
@@ -297,10 +306,10 @@
             gc[t, k].wait_recv()
 
 
-def write_out(*refs):
-    count = (len(refs) - 1) // 2
-    sem = refs[-1]
-    copies = [pltpu.make_async_copy(refs[k], refs[count + k], sem.at[k]) for k in range(count)]
+def write_out(nz, new, row, col, full, new_out, row_out, col_out, full_out, sem):
+    pairs = [(full.at[a, b, u], full_out.at[a, b, u]) for a in range(2) for b in range(2) for u in range(nz)]
+    pairs += [(new, new_out), (row, row_out), (col, col_out)]
+    copies = [pltpu.make_async_copy(src, dst, sem.at[k]) for k, (src, dst) in enumerate(pairs)]
     for copy in copies:
         copy.start()
     for copy in copies:
@@ -345,11 +354,11 @@
             collective_id=0, has_side_effects=True, vmem_limit_bytes=VMEM_BYTES - held),
     )(grad_bucket.reshape(2, 2, nz, 2, rows, columns), parameters[0], row_state, column_state)
     new, row, col, full = pl.pallas_call(
-        write_out,
+        functools.partial(write_out, nz),
         out_shape=tuple(jax.ShapeDtypeStruct(*shape) for shape in shapes),
         in_specs=[vmem] * 4,
         out_specs=(hbm,) * 4,
-        scratch_shapes=[dma((4,))],
+        scratch_shapes=[dma((4 * nz + 3,))],
         compiler_params=pltpu.CompilerParams(vmem_limit_bytes=4 * 1024 * 1024),
     )(*[pltpu.with_memory_space_constraint(result, pltpu.VMEM) for result in results])
     return (new[None], row, col, full.reshape(full_width, columns))

time: 88 us -> 87.9 us (level)
  no operation moved by 1% of the time
where the time goes in v3:
time: 87.9 us; the launch traced here: 87.8 us
  Pallas kernels  87.1 us (99%)
    pallas_call x1, Pallas kernels, fused(): pl.pallas_call(functools.partial(kernel, nx, nz), out_shape=tuple((pltpu....  83.9 us
    pallas_call x1, Pallas kernels, fused(): pl.pallas_call(functools.partial(write_out, nz), out_shape=tuple((jax.Sha...  3.2 us

profile of v3, /device:TPU:0, one launch (start us, length us, event | category | flops | bytes accessed | tf_op | source)
XLA Modules:
  0.0 87.8 jit_solution(10259131156885030404)
XLA Ops:
  0.6 83.9 %shard_map.75 = (bf16[112,1024]{1,0:T(8,128)(2,1)S(1)}, f32[1,112]{1,0:T(1,128)S(1)}, f32[1,1024]{1,0:T(1,128)S(1)}, bf16[2,2,4,2,112,1024]{5,4,3,2,1,0:T(8,128)(2,1)S(1)}) custom-call(bf16[2,2,4,2,112,1024]{5,4,3,2,1,0:T(8,128)(2,1)} %bitcast.4, bf16[112,1024]{1,0:T(8,128)(2,1)} %bitcast.5, f32[1,112]{1,0:T(1,128)} %row_in.1, f32[1,1024]{1,0:T(1,128)} %col_in.1), custom_call_target="tpu_custom_call" | custom-call | tf_op jit(solution)/shard_map/pallas_call | solution.py:329
  84.6 3.2 %shard_map.76 = (bf16[112,1024]{1,0:T(8,128)(2,1)}, f32[1,112]{1,0:T(1,128)}, f32[1,1024]{1,0:T(1,128)}, bf16[2,2,4,2,112,1024]{5,4,3,2,1,0:T(8,128)(2,1)}) custom-call(bf16[112,1024]{1,0:T(8,128)(2,1)S(1)} %get-tuple-element.12.new, f32[1,112]{1,0:T(1,128)S(1)} %get-tuple-element.13.row, f32[1,1024]{1,0:T(1,128)S(1)} %get-tuple-element.14.col, ...), custom_call_target="tpu_custom_call" | custom-call | tf_op jit(solution)/shard_map/pallas_call | solution.py:356

commit v4 on v3

--- a/solution.py
+++ b/solution.py
@@ -107,7 +107,7 @@
         return total
 
     def over_rows(step):
-        @pl.loop(0, tiles)
+        @pl.loop(0, tiles, unroll=True)
         def _(i):
             step(pl.ds(pl.multiple_of(i * TILE, TILE), TILE))
 

time: 87.9 us -> 87.4 us (level)
  no operation moved by 1% of the time
where the time goes in v4:
time: 87.4 us; the launch traced here: 87.2 us
  Pallas kernels  86.6 us (99%)
    pallas_call x1, Pallas kernels, fused(): pl.pallas_call(functools.partial(kernel, nx, nz), out_shape=tuple((pltpu....  83.4 us
    pallas_call x1, Pallas kernels, fused(): pl.pallas_call(functools.partial(write_out, nz), out_shape=tuple((jax.Sha...  3.2 us

profile of v4, /device:TPU:0, one launch (start us, length us, event | category | flops | bytes accessed | tf_op | source)
XLA Modules:
  0.0 87.2 jit_solution(2719305460358889110)
XLA Ops:
  0.6 83.4 %shard_map.75 = (bf16[112,1024]{1,0:T(8,128)(2,1)S(1)}, f32[1,112]{1,0:T(1,128)S(1)}, f32[1,1024]{1,0:T(1,128)S(1)}, bf16[2,2,4,2,112,1024]{5,4,3,2,1,0:T(8,128)(2,1)S(1)}) custom-call(bf16[2,2,4,2,112,1024]{5,4,3,2,1,0:T(8,128)(2,1)} %bitcast.4, bf16[112,1024]{1,0:T(8,128)(2,1)} %bitcast.5, f32[1,112]{1,0:T(1,128)} %row_in.1, f32[1,1024]{1,0:T(1,128)} %col_in.1), custom_call_target="tpu_custom_call" | custom-call | tf_op jit(solution)/shard_map/pallas_call | solution.py:329
  84.0 3.2 %shard_map.76 = (bf16[112,1024]{1,0:T(8,128)(2,1)}, f32[1,112]{1,0:T(1,128)}, f32[1,1024]{1,0:T(1,128)}, bf16[2,2,4,2,112,1024]{5,4,3,2,1,0:T(8,128)(2,1)}) custom-call(bf16[112,1024]{1,0:T(8,128)(2,1)S(1)} %get-tuple-element.12.new, f32[1,112]{1,0:T(1,128)S(1)} %get-tuple-element.13.row, f32[1,1024]{1,0:T(1,128)S(1)} %get-tuple-element.14.col, ...), custom_call_target="tpu_custom_call" | custom-call | tf_op jit(solution)/shard_map/pallas_call | solution.py:356
